TPU v7x, 32 devices: a whole 2x2x4 slice. The times are simulated.
32 devices in a mesh: section: 4 (over z), tensor: 4 (over y, x), dp: 2 (over core).
Axes of the slice: x: 2, y: 2, z: 4, core: 2. Of those that a mesh axis runs over, the one named last changes fastest.
Arguments:
- forward_rows: bfloat16 [4, 2, 192, 8192], P('section', 'dp', None, 'tensor'), may hold values from -6 to 6
- saved_rows: bfloat16 [4, 2, 192, 8192], P('section', 'dp', None, 'tensor'), may hold values from -40.5 to 40.5
- output_grad: bfloat16 [4, 2, 192, 8192], P('section', 'dp', None, 'tensor'), may hold values from -1.27 to 1.27
- lengths: int32 [4, 2, 2], P('section', 'dp'), may hold values from 1 to 96
- norm_gain: bfloat16 [4, 8192], P('section', 'tensor'), may hold values from 0.5 to 1.5
- down_map: bfloat16 [4, 192, 8192], P('section', None, 'tensor'), may hold values from -0.067396115 to 0.067396115
- up_map: bfloat16 [4, 192, 8192], P('section', None, 'tensor'), may hold values from -1.0625 to 1.0625
Outputs:
- next_inputs: bfloat16 [4, 2, 192, 8192], P('section', 'dp', None, 'tensor')
- next_grads: bfloat16 [4, 2, 192, 8192], P('section', 'dp', None, 'tensor')
- grad_down: bfloat16 [4, 192, 8192], P('section', 'dp', 'tensor')
- grad_up: bfloat16 [4, 192, 8192], P('section', 'dp', 'tensor')
All inputs are finite; a program needn't handle non-finite values.
Results may differ from a plain program's by a relative error of at most 0.02.
Values may be sent and summed in bfloat16 or wider, within the bound.
A program may use at most 64 MiB of HBM per device.

v0:
```python
import functools

import jax
import jax.numpy as jnp
from jax import lax
from jax.experimental import pallas as pl
from jax.experimental.pallas import tpu as pltpu
from jax.sharding import PartitionSpec as P

EPSILON = 1e-05
LANES = 128
RAW_FORWARD = 0.375
RAW_BACK = 0.125
BLOCKS = 4
F32 = jnp.float32
BF16 = jnp.bfloat16


def contract_last(left_side, right_side):
    return lax.dot_general(
        left_side, right_side, (((1,), (1,)), ((), ())), preferred_element_type=F32
    )


def contract_rows(left_side, right_side):
    return lax.dot_general(
        left_side, right_side, (((0,), (0,)), ((), ())), preferred_element_type=F32
    )


def flip(index, bit):
    step = 1 << bit
    return index + step * (1 - 2 * ((index // step) % 2))


def tick(sizes, fwd_hbm, sav_hbm, grad_hbm, len_ref, gain_ref, down_hbm, up_hbm,
         next_in, next_gr, grad_down, grad_up,
         fwd, sav, kept, down, up, scaled,
         acc_f, acc_b, send_f, recv_f, send_b, recv_b, out_f, out_b,
         part, part_recv, act_out, act_in, back_out, back_in,
         side_out, side_in, sq_out, sq_in, sq_send_sem, sq_recv_sem,
         raw_fwd, raw_up, raw_sav, raw_grad, raw_down, raw_gain, load_sem,
         f_send_sem, f_recv_sem, b_send_sem, b_recv_sem,
         sec_send_sem, sec_recv_sem, dp_send_sem, dp_recv_sem,
         raw_send_sem, raw_recv_sem, relay_send_sem, relay_recv_sem):
    n_sec, n_ten, n_dp, chunk = sizes
    rows, width = fwd.shape
    rank = down.shape[0]
    full_width = width * n_ten
    n_seq = len_ref.shape[1]
    bits = n_ten.bit_length() - 1
    half = rows // 2
    n_chunk = width // chunk
    share = rank // n_dp
    sec, ten, dp = lax.axis_index("section"), lax.axis_index("tensor"), lax.axis_index("dp")

    loads = [
        pltpu.make_async_copy(src, dst, load_sem.at[i])
        for i, (src, dst) in enumerate(
            ((fwd_hbm, fwd), (down_hbm, down), (sav_hbm, sav), (grad_hbm, kept), (up_hbm, up))
        )
    ]
    for i in (2, 1, 3, 4, 0):
        loads[i].start()

    barrier = pltpu.get_barrier_semaphore()
    for k in range(1, n_ten):
        pl.semaphore_signal(barrier, inc=1, device_id={"tensor": (ten + k) % n_ten})
    for k in range(1, n_dp):
        pl.semaphore_signal(barrier, inc=1, device_id={"dp": (dp + k) % n_dp})

    @pl.when(sec > 0)
    def _():
        pl.semaphore_signal(barrier, inc=1, device_id={"section": sec - 1})

    @pl.when(sec < n_sec - 1)
    def _():
        pl.semaphore_signal(barrier, inc=1, device_id={"section": sec + 1})

    columns = [slice(c * chunk, (c + 1) * chunk) for c in range(n_chunk)]
    raw_f, raw_b = raw_fwd.shape[1], raw_sav.shape[1]
    mine = pl.ds(pl.multiple_of(dp * share, share), share)
    tail_f, tail_b = pl.ds(width - raw_f, raw_f), pl.ds(width - raw_b, raw_b)

    def across(i, source, target, step):
        return pltpu.make_async_remote_copy(
            src_ref=source,
            dst_ref=target,
            send_sem=raw_send_sem.at[i],
            recv_sem=raw_recv_sem.at[i],
            device_id={"section": sec + step},
        )

    raw_ups = across(0, up_hbm.at[mine, tail_f], raw_up.at[mine], 1)
    raw_fwds = across(1, fwd_hbm.at[:, tail_f], raw_fwd, 1)
    acts = across(2, act_out, act_in, 1)
    raw_downs = across(3, down_hbm.at[mine, tail_b], raw_down.at[mine], -1)
    raw_gains = across(4, gain_ref, raw_gain, -1)
    raw_savs = across(5, sav_hbm.at[:, tail_b], raw_sav, -1)
    raw_grads = across(6, grad_hbm.at[:, tail_b], raw_grad, -1)
    backs = across(7, back_out, back_in, -1)
    sides = across(8, side_out, side_in, -1)
    up_way, down_way = (raw_ups, raw_fwds, acts), (raw_downs, raw_gains, raw_savs, raw_grads, backs, sides)

    def relay(way, k):
        ref = (raw_up, raw_down)[way].at[mine]
        return pltpu.make_async_remote_copy(
            src_ref=ref,
            dst_ref=ref,
            send_sem=relay_send_sem.at[way, k - 1],
            recv_sem=relay_recv_sem.at[way, k - 1],
            device_id={"dp": (dp + k) % n_dp},
        )

    pl.semaphore_wait(barrier, n_ten - 1 + n_dp - 1 + jnp.where(sec > 0, 1, 0) + jnp.where(sec < n_sec - 1, 1, 0))

    @pl.when(sec < n_sec - 1)
    def _():
        for copy in up_way[:-1]:
            copy.start()

    @pl.when(sec > 0)
    def _():
        for copy in down_way[:-2]:
            copy.start()

    def exchange(form, q, p):
        acc, send, recv, send_sem, recv_sem, blocks = form
        span = pl.ds(q * (rows // blocks), rows // blocks)
        return pltpu.make_async_remote_copy(
            src_ref=send.at[p, span],
            dst_ref=recv.at[p, span],
            send_sem=send_sem.at[q, p],
            recv_sem=recv_sem.at[q, p],
            device_id={"tensor": flip(ten, (q + p) % bits)},
        )

    form_f = (acc_f, send_f, recv_f, f_send_sem, f_recv_sem, 2)
    form_b = (acc_b, send_b, recv_b, b_send_sem, b_recv_sem, BLOCKS)

    def begin(form, q, p):
        acc, send, blocks = form[0], form[1], form[5]
        span = pl.ds(q * (rows // blocks), rows // blocks)
        send[p, span] = acc[span].astype(BF16)
        exchange(form, q, p).start()

    def finish(form, q, p):
        acc, recv, blocks = form[0], form[2], form[5]
        span = pl.ds(q * (rows // blocks), rows // blocks)
        exchange(form, q, p).wait()
        acc[span] = acc[span] + recv[p, span].astype(F32)

    eye = lax.broadcasted_iota(jnp.int32, (rows, rows), 0) == lax.broadcasted_iota(jnp.int32, (rows, rows), 1)

    def to_row(column):
        return jnp.sum(jnp.where(eye, column, 0.0), axis=0, keepdims=True)

    def to_column(row):
        return jnp.sum(jnp.where(eye, row, 0.0), axis=1, keepdims=True)

    def squares(i, k):
        return pltpu.make_async_remote_copy(
            src_ref=sq_out.at[i],
            dst_ref=sq_in.at[i, k - 1],
            send_sem=sq_send_sem.at[i, k - 1],
            recv_sem=sq_recv_sem.at[i, k - 1],
            device_id={"tensor": (ten + k) % n_ten},
        )

    def spread(i, column):
        sq_out[i] = jnp.broadcast_to(to_row(column), (8, rows))
        for k in range(1, n_ten):
            squares(i, k).start()

    def scale_of(i):
        row = sq_out[i, 0:1]
        for k in range(1, n_ten):
            squares(i, k).wait()
            row += sq_in[i, k - 1, 0:1]
        return lax.rsqrt(to_column(row) / full_width + EPSILON)

    load_fwd, load_down, load_sav, load_grad, load_up = loads
    load_sav.wait()
    square_s = jnp.zeros((rows, 1), F32)
    for cols in columns:
        values = sav[:, cols].astype(F32)
        square_s += jnp.sum(values * values, axis=1, keepdims=True)
        scaled[:, cols] = (values * gain_ref[:, cols].astype(F32)).astype(BF16)
    spread(0, square_s)
    load_down.wait()
    total_s = jnp.zeros((rows, rank), F32)
    for cols in columns:
        total_s += contract_last(scaled[:, cols], down[:, cols])
    load_grad.wait()
    load_up.wait()
    position = lax.broadcasted_iota(jnp.int32, (rows, 1), 0)
    seq_rows = rows // n_seq
    limit = jnp.full((rows, 1), 0, jnp.int32)
    for i in range(n_seq):
        limit = jnp.where(position >= i * seq_rows, i * seq_rows + len_ref[0, i], limit)
    keep = position < limit
    total_g = jnp.zeros((rows, rank), F32)
    for cols in columns:
        held = jnp.where(keep, kept[:, cols].astype(F32), 0.0).astype(BF16)
        kept[:, cols] = held
        total_g += contract_last(held, up[:, cols])
    acc_b[...] = jnp.concatenate([total_g, total_s], axis=1)
    if bits:
        for q in range(BLOCKS):
            begin(form_b, q, 0)

    load_fwd.wait()
    total = jnp.zeros((rows, rank), F32)
    square_f = jnp.zeros((rows, 1), F32)
    for cols in columns:
        values = fwd[:, cols].astype(F32)
        square_f += jnp.sum(values * values, axis=1, keepdims=True)
        gained = (values * gain_ref[:, cols].astype(F32)).astype(BF16)
        total += contract_last(gained, down[:, cols])
    acc_f[...] = total
    spread(1, square_f)
    if bits:
        for q in range(2):
            begin(form_f, q, 0)
    for p in range(1, bits):
        for q in range(BLOCKS):
            finish(form_b, q, p - 1)
            begin(form_b, q, p)
        for q in range(2):
            finish(form_f, q, p - 1)
            begin(form_f, q, p)

    done_f = [slice(a, min(a + chunk, width - raw_f)) for a in range(0, width - raw_f, chunk)]
    done_b = [slice(a, min(a + chunk, width - raw_b)) for a in range(0, width - raw_b, chunk)]

    def shift(way, source, target, g, c):
        cols = (done_f, done_b)[way][c]
        span = pl.ds(cols.start, cols.stop - cols.start)
        part_rows = pl.ds(g * half, half)
        return pltpu.make_async_remote_copy(
            src_ref=source.at[part_rows, span],
            dst_ref=target.at[part_rows, span],
            send_sem=sec_send_sem.at[way, g, c],
            recv_sem=sec_recv_sem.at[way, g, c],
            device_id={"section": sec + 1 if way == 0 else sec - 1},
        )

    def shifts(way):
        source, target = ((out_f, next_in), (out_b, next_gr))[way]
        return [shift(way, source, target, g, c) for g in range(2) for c in range(len((done_f, done_b)[way]))]

    scale_s = scale_of(0)
    acts_s, backs_s, tilts = [], [], []
    for g in range(2):
        span = slice(g * half, (g + 1) * half)
        if bits:
            for q in range(g * BLOCKS // 2, (g + 1) * BLOCKS // 2):
                finish(form_b, q, bits - 1)
        own_scale = scale_s[span]
        slope = acc_b[span, :rank]
        rank_s = acc_b[span, rank:] * own_scale
        gate = jax.nn.sigmoid(rank_s)
        acts_s.append((rank_s * gate).astype(BF16))
        back = slope * (gate * (1.0 + rank_s * (1.0 - gate)))
        tilt = jnp.sum(back.astype(BF16).astype(F32) * rank_s, axis=1, keepdims=True) * (own_scale * own_scale / full_width)
        back_s = back * own_scale
        back_rows = back_s.astype(BF16)
        backs_s.append(back_s)
        tilts.append(tilt)

        @pl.when(sec > 0)
        def _():
            if g == 1:
                back_out[...] = jnp.concatenate(backs_s, axis=1).astype(BF16)
                top = lax.broadcasted_iota(jnp.int32, (8, rows), 0) == 0
                side_out[...] = jnp.where(
                    top, to_row(jnp.concatenate(tilts, axis=0)), to_row(jnp.where(keep, 1.0, 0.0))
                )
                backs.start()
                sides.start()
            for c, cols in enumerate(done_b):
                normed = jnp.dot(back_rows, down[:, cols], preferred_element_type=F32)
                out_b[span, cols] = (
                    kept[span, cols].astype(F32)
                    + gain_ref[:, cols].astype(F32) * normed
                    - sav[span, cols].astype(F32) * tilt
                ).astype(BF16)
                shift(1, out_b, next_gr, g, c).start()

    back_scaled = jnp.concatenate(backs_s, axis=0).astype(BF16)
    act_s = jnp.concatenate(acts_s, axis=0)

    scale_f = scale_of(1)
    if bits:
        for q in range(2):
            finish(form_f, q, bits - 1)
    rank_f = acc_f[...] * scale_f
    act_f = rank_f * jax.nn.sigmoid(rank_f)

    @pl.when(sec < n_sec - 1)
    def _():
        act_out[...] = jnp.concatenate([act_f[:half], act_f[half:]], axis=1).astype(BF16)
        acts.start()

    act_f = act_f.astype(BF16)

    @pl.when(sec < n_sec - 1)
    def _():
        for c, cols in enumerate(done_f):
            grown = jnp.dot(act_f, up[:, cols], preferred_element_type=F32)
            out_f[:, cols] = (fwd[:, cols].astype(F32) + grown).astype(BF16)
            for g in range(2):
                shift(0, out_f, next_in, g, c).start()

    def trade(i, k):
        target = (dp + k) % n_dp
        return pltpu.make_async_remote_copy(
            src_ref=part.at[i, pl.ds(pl.multiple_of(target * share, share), share)],
            dst_ref=part_recv.at[i, k - 1],
            send_sem=dp_send_sem.at[i, k - 1],
            recv_sem=dp_recv_sem.at[i, k - 1],
            device_id={"dp": target},
        )

    for i, (left_side, right_side) in enumerate(((back_scaled, scaled), (act_s, kept))):
        for cols in columns:
            part[i, :, cols] = contract_rows(left_side, right_side[:, cols]).astype(BF16)
        for k in range(1, n_dp):
            trade(i, k).start()

    @pl.when(sec > 0)
    def _():
        raw_ups.wait_recv()
        for k in range(1, n_dp):
            relay(0, k).start()

    @pl.when(sec < n_sec - 1)
    def _():
        raw_downs.wait_recv()
        for k in range(1, n_dp):
            relay(1, k).start()

    for i, out in enumerate((grad_down, grad_up)):
        for k in range(1, n_dp):
            trade(i, k).wait()
        for cols in columns:
            summed = part[i, mine, cols].astype(F32)
            for k in range(1, n_dp):
                summed += part_recv[i, k - 1, :, cols].astype(F32)
            out[:, cols] = (summed * (1.0 / n_dp)).astype(BF16)

    @pl.when(sec == 0)
    def _():
        next_in[...] = jnp.zeros_like(next_in)

    @pl.when(sec == n_sec - 1)
    def _():
        next_gr[...] = jnp.zeros_like(next_gr)

    @pl.when(sec > 0)
    def _():
        for k in range(1, n_dp):
            relay(0, k).wait()
        raw_fwds.wait_recv()
        acts.wait_recv()
        came = act_in[...].astype(F32)
        came = jnp.concatenate([came[:, :rank], came[:, rank:]], axis=0).astype(BF16)
        for a in range(0, raw_f, chunk):
            b = min(a + chunk, raw_f)
            grown = jnp.dot(came, raw_up[:, a:b], preferred_element_type=F32)
            next_in[:, width - raw_f + a:width - raw_f + b] = (raw_fwd[:, a:b].astype(F32) + grown).astype(BF16)

    @pl.when(sec < n_sec - 1)
    def _():
        for k in range(1, n_dp):
            relay(1, k).wait()
        raw_gains.wait_recv()
        raw_savs.wait_recv()
        raw_grads.wait_recv()
        backs.wait_recv()
        sides.wait_recv()
        came = back_in[...].astype(F32)
        far_back = jnp.concatenate([came[:, :rank], came[:, rank:]], axis=0).astype(BF16)
        far_tilt = to_column(side_in[0:1])
        far_keep = to_column(side_in[1:2])
        for a in range(0, raw_b, chunk):
            b = min(a + chunk, raw_b)
            cols = slice(width - raw_b + a, width - raw_b + b)
            normed = jnp.dot(far_back, raw_down[:, a:b], preferred_element_type=F32)
            next_gr[:, cols] = (
                jnp.where(far_keep > 0.5, raw_grad[:, a:b].astype(F32), 0.0)
                + raw_gain[:, cols].astype(F32) * normed
                - raw_sav[:, a:b].astype(F32) * far_tilt
            ).astype(BF16)

    @pl.when(sec < n_sec - 1)
    def _():
        for copy in up_way:
            copy.wait_send()
        for copy in shifts(0):
            copy.wait_send()
        for copy in shifts(1):
            copy.wait_recv()

    @pl.when(sec > 0)
    def _():
        for copy in down_way:
            copy.wait_send()
        for copy in shifts(1):
            copy.wait_send()
        for copy in shifts(0):
            copy.wait_recv()


def place(*refs):
    count = len(refs) // 2
    sems = refs[-1]
    copies = [pltpu.make_async_copy(refs[i], refs[count + i], sems.at[i]) for i in range(count)]
    for copy in copies:
        copy.start()
    for copy in copies:
        copy.wait()


def solution(mesh):
    n_sec, n_ten, n_dp = (mesh.shape[name] for name in ("section", "tensor", "dp"))

    def shards(forward_rows, saved_rows, output_grad, lengths, norm_gain, down_map, up_map):
        rows, width = forward_rows.shape[2:]
        rank = down_map.shape[1]
        share = rank // n_dp
        bits = n_ten.bit_length() - 1
        chunk = min(width, 4 * LANES)
        n_chunk = width // chunk
        raw_f = int(width * RAW_FORWARD) // LANES * LANES
        raw_b = int(width * RAW_BACK) // LANES * LANES
        peers = max(n_ten - 1, 1)
        steps = max(bits, 1)
        vmem = pl.BlockSpec(memory_space=pltpu.VMEM)
        anywhere = pl.BlockSpec(memory_space=pl.ANY)
        flops = 7 * 2 * rows * rank * width
        dma = pltpu.SemaphoreType.DMA
        shapes = ((rows, width),) * 2 + ((share, width),) * 2
        results = pl.pallas_call(
            functools.partial(tick, (n_sec, n_ten, n_dp, chunk)),
            out_shape=tuple(pltpu.VMEM(shape, BF16) for shape in shapes),
            in_specs=[anywhere, anywhere, anywhere, pl.BlockSpec(memory_space=pltpu.SMEM), vmem, anywhere, anywhere],
            out_specs=(vmem,) * 4,
            scratch_shapes=[
                pltpu.VMEM((rows, width), BF16),
                pltpu.VMEM((rows, width), BF16),
                pltpu.VMEM((rows, width), BF16),
                pltpu.VMEM((rank, width), BF16),
                pltpu.VMEM((rank, width), BF16),
                pltpu.VMEM((rows, width), BF16),
                pltpu.VMEM((rows, rank), F32),
                pltpu.VMEM((rows, 2 * rank), F32),
                pltpu.VMEM((steps, rows, rank), BF16),
                pltpu.VMEM((steps, rows, rank), BF16),
                pltpu.VMEM((steps, rows, 2 * rank), BF16),
                pltpu.VMEM((steps, rows, 2 * rank), BF16),
                pltpu.VMEM((rows, width), BF16),
                pltpu.VMEM((rows, width), BF16),
                pltpu.VMEM((2, rank, width), BF16),
                pltpu.VMEM((2, max(n_dp - 1, 1), share, width), BF16),
                pltpu.VMEM((rows // 2, 2 * rank), BF16),
                pltpu.VMEM((rows // 2, 2 * rank), BF16),
                pltpu.VMEM((rows // 2, 2 * rank), BF16),
                pltpu.VMEM((rows // 2, 2 * rank), BF16),
                pltpu.VMEM((8, rows), F32),
                pltpu.VMEM((8, rows), F32),
                pltpu.VMEM((2, 8, rows), F32),
                pltpu.VMEM((2, peers, 8, rows), F32),
                dma((2, peers)),
                dma((2, peers)),
                pltpu.VMEM((rows, raw_f), BF16),
                pltpu.VMEM((rank, raw_f), BF16),
                pltpu.VMEM((rows, raw_b), BF16),
                pltpu.VMEM((rows, raw_b), BF16),
                pltpu.VMEM((rank, raw_b), BF16),
                pltpu.VMEM((1, width), BF16),
                dma((5,)),
                dma((2, steps)),
                dma((2, steps)),
                dma((BLOCKS, steps)),
                dma((BLOCKS, steps)),
                dma((2, 2, n_chunk)),
                dma((2, 2, n_chunk)),
                dma((2, max(n_dp - 1, 1))),
                dma((2, max(n_dp - 1, 1))),
                dma((9,)),
                dma((9,)),
                dma((2, max(n_dp - 1, 1))),
                dma((2, max(n_dp - 1, 1))),
            ],
            compiler_params=pltpu.CompilerParams(collective_id=0, has_side_effects=True),
            cost_estimate=pl.CostEstimate(
                flops=flops, bytes_accessed=16 * rows * width, transcendentals=4 * rows * rank
            ),
            name="tick",
        )(
            forward_rows[0, 0], saved_rows[0, 0], output_grad[0, 0], lengths[0], norm_gain, down_map[0], up_map[0]
        )
        next_inputs, next_grads, grad_down, grad_up = pl.pallas_call(
            place,
            out_shape=tuple(jax.ShapeDtypeStruct(shape, BF16) for shape in shapes),
            in_specs=[vmem] * 4,
            out_specs=(anywhere,) * 4,
            scratch_shapes=[dma((4,))],
            name="place",
        )(*[pltpu.with_memory_space_constraint(x, pltpu.VMEM) for x in results])
        return next_inputs[None, None], next_grads[None, None], grad_down[None], grad_up[None]

    row_spec = P("section", "dp", None, "tensor")
    map_spec = P("section", None, "tensor")
    part_spec = P("section", "dp", "tensor")
    return jax.shard_map(
        shards,
        mesh=mesh,
        in_specs=(row_spec, row_spec, row_spec, P("section", "dp"), P("section", "tensor"), map_spec, map_spec),
        out_specs=(row_spec, row_spec, part_spec, part_spec),
        check_vma=False,
    )
```

profile of v0, /device:TPU:0, one launch (start us, length us, event | category | flops | bytes accessed | tf_op | source)
XLA Modules:
  0.0 32.9 jit_solution(17782201929564729585)
XLA Ops:
  0.6 30.9 %tick.1 = (bf16[192,2048]{1,0:T(8,128)(2,1)S(1)}, bf16[192,2048]{1,0:T(8,128)(2,1)S(1)}, bf16[96,2048]{1,0:T(8,128)(2,1)S(1)}, bf16[96,2048]{1,0:T(8,128)(2,1)S(1)}) custom-call(bf16[192,2048]{1,0:T(8,128)(2,1)} %bitcast.10, bf16[192,2048]{1,0:T(8,128)(2,1)} %bitcast.11, bf16[192,2048]{1,0:T(8,128)(2,1)} %bitcast.12, s32[1,2]{1,0:T(1,128)} %bitcast.15, ...), custom_call_target="tpu_custom_call" | custom-call | flops 1056964608 | bytes 6291456 | tf_op jit(solution)/shard_map/tick/pallas_call | solution.py:444
  31.5 1.4 %place.1 = (bf16[192,2048]{1,0:T(8,128)(2,1)}, bf16[192,2048]{1,0:T(8,128)(2,1)}, bf16[96,2048]{1,0:T(8,128)(2,1)}, bf16[96,2048]{1,0:T(8,128)(2,1)}) custom-call(bf16[192,2048]{1,0:T(8,128)(2,1)S(1)} %get-tuple-element.12.refs_0_, bf16[192,2048]{1,0:T(8,128)(2,1)S(1)} %get-tuple-element.13.refs_1_, bf16[96,2048]{1,0:T(8,128)(2,1)S(1)} %get-tuple-element.14.refs_2_, ...), custom_call_target="tpu_custom_call" | custom-call | tf_op jit(solution)/shard_map/place/pallas_call | solution.py:504
where the time goes:
time: 33.2 us; the launch traced here: 32.9 us
  Pallas kernels  32.3 us (97%)
  between operations  0.64 us (2%)
    pallas_call x1, Pallas kernels, shards(): pl.pallas_call(functools.partial(tick, (n_sec, n_ten, n_dp, chunk)), out_...  30.9 us
    pallas_call x1, Pallas kernels, shards(): pl.pallas_call(place, out_shape=tuple((jax.ShapeDtypeStruct(shape, BF16)...  1.43 us

commit v1 on v0

v1 whole, which is shorter than its diff:
```python
import functools

import jax
import jax.numpy as jnp
from jax import lax
from jax.experimental import pallas as pl
from jax.experimental.pallas import tpu as pltpu
from jax.sharding import PartitionSpec as P

EPSILON = 1e-05
LANES = 128
RAW_FORWARD = 0.375
RAW_BACK = 0.125
F32 = jnp.float32
BF16 = jnp.bfloat16


def contract_last(left_side, right_side):
    return lax.dot_general(
        left_side, right_side, (((1,), (1,)), ((), ())), preferred_element_type=F32
    )


def contract_rows(left_side, right_side):
    return lax.dot_general(
        left_side, right_side, (((0,), (0,)), ((), ())), preferred_element_type=F32
    )


def flip(index, bit):
    step = 1 << bit
    return index + step * (1 - 2 * ((index // step) % 2))


def row_groups(rows):
    sizes = (rows // 6, rows // 3, rows // 2) if rows % 192 == 0 else (rows,)
    starts = [sum(sizes[:i]) for i in range(len(sizes))]
    return list(zip(starts, sizes))


def semaphores(n_group, bits, n_dp):
    names = ["len", "gain", "sav", "down", "grad", "up", "fwd"]
    names += [("sq", kind, p) for kind in "sr" for p in range(bits)]
    names += [("b", g, p) for g in range(n_group) for p in range(bits)] + ["b_send"]
    names += [("f", p) for p in range(bits)] + ["f_send"]
    names += [(side, kind) for side in ("out_f", "out_b") for kind in "sr"]
    names += [(side, kind) for side in ("raw_up", "raw_down", "raw_gain", "act", "back") for kind in "sr"]
    names += ["raw_fwd_r", "raw_sav_s", "raw_pair_r"]
    names += [("all", kind, p) for kind in "sr" for p in range(bits)]
    names += [("trade", kind, k) for kind in "sr" for k in range(1, n_dp)]
    names += [("relay", way, kind, k) for way in range(2) for kind in "sr" for k in range(1, n_dp)]
    return {name: i for i, name in enumerate(names)}


def tick(sizes, fwd_hbm, sav_hbm, grad_hbm, len_hbm, gain_hbm, down_hbm, up_hbm,
         next_in, next_gr, grad_down, grad_up,
         lens, gain, fwd, sav, kept, down, up, scaled,
         acc_f, acc_b, send_f, recv_f, send_b, recv_b, out_f, out_b,
         part, part_recv, act_out, back_out, pair, sq_out, sq_in,
         raw_fwd, raw_up, raw_pair, raw_down, raw_gain, sems):
    n_sec, n_ten, n_dp, chunk = sizes
    rows, width = fwd.shape
    rank = down.shape[0]
    padded = act_out.shape[1]
    full_width = width * n_ten
    n_seq = lens.shape[1]
    bits = n_ten.bit_length() - 1
    share = rank // n_dp
    quarter = rows // n_ten
    groups = row_groups(rows)
    index = semaphores(len(groups), bits, n_dp)
    sec, ten, dp = lax.axis_index("section"), lax.axis_index("tensor"), lax.axis_index("dp")

    def sem(*name):
        return sems.at[index[name if len(name) > 1 else name[0]]]

    loads = {
        name: pltpu.make_async_copy(source, target, sem(name))
        for name, source, target in (
            ("sav", sav_hbm, sav), ("gain", gain_hbm, gain), ("down", down_hbm, down), ("len", len_hbm, lens),
            ("grad", grad_hbm, kept), ("up", up_hbm, up), ("fwd", fwd_hbm, fwd),
        )
    }
    for load in loads.values():
        load.start()

    @pl.when(sec == 0)
    def _():
        pair[:, :padded] = jnp.zeros((rows, padded), BF16)

    @pl.when(sec == n_sec - 1)
    def _():
        pair[:, padded:] = jnp.zeros((rows, padded), BF16)

    barrier = pltpu.get_barrier_semaphore()
    for p in range(bits):
        pl.semaphore_signal(barrier, inc=1, device_id={"tensor": flip(ten, p)})
    for k in range(1, n_dp):
        pl.semaphore_signal(barrier, inc=1, device_id={"dp": (dp + k) % n_dp})

    @pl.when(sec > 0)
    def _():
        pl.semaphore_signal(barrier, inc=1, device_id={"section": sec - 1})

    @pl.when(sec < n_sec - 1)
    def _():
        pl.semaphore_signal(barrier, inc=1, device_id={"section": sec + 1})

    columns = [slice(c, c + chunk) for c in range(0, width, chunk)]
    raw_f, raw_b = raw_fwd.shape[1], raw_pair.shape[2]
    mine = pl.ds(pl.multiple_of(dp * share, share), share)
    own = pl.ds(pl.multiple_of(ten * quarter, quarter), quarter)
    tail_f, tail_b = pl.ds(width - raw_f, raw_f), pl.ds(width - raw_b, raw_b)

    def remote(source, target, send, recv, **place):
        return pltpu.make_async_remote_copy(
            src_ref=source, dst_ref=target, send_sem=send, recv_sem=recv, device_id=place
        )

    def across(step, source, target, send, recv):
        return remote(source, target, send, recv, section=sec + step)

    raw_ups = across(1, up.at[mine, tail_f], raw_up.at[mine], sem("raw_up", "s"), sem("raw_up", "r"))
    raw_fwds = across(1, fwd.at[:, tail_f], raw_fwd, sem("out_f", "s"), sem("raw_fwd_r"))
    acts = across(1, act_out.at[own], pair.at[own, pl.ds(0, padded)], sem("act", "s"), sem("act", "r"))
    raw_downs = across(-1, down.at[mine, tail_b], raw_down.at[mine], sem("raw_down", "s"), sem("raw_down", "r"))
    raw_gains = across(-1, gain.at[:, tail_b], raw_gain, sem("raw_gain", "s"), sem("raw_gain", "r"))
    raw_savs = across(-1, sav.at[:, tail_b], raw_pair.at[0], sem("raw_sav_s"), sem("raw_pair_r"))
    raw_keeps = across(-1, kept.at[:, tail_b], raw_pair.at[1], sem("out_b", "s"), sem("raw_pair_r"))
    raw_pairs = across(-1, raw_pair, raw_pair, sem("raw_sav_s"), sem("raw_pair_r"))
    backs = across(-1, back_out.at[own], pair.at[own, pl.ds(padded, padded)], sem("back", "s"), sem("back", "r"))

    def relay(way, k):
        ref = (raw_up, raw_down)[way].at[mine]
        return remote(ref, ref, sem("relay", way, "s", k), sem("relay", way, "r", k), dp=(dp + k) % n_dp)

    def exchange_b(start, size, g, p):
        for q in range(2):
            span = pl.ds(start + q * (size // 2), size // 2)
            remote(
                send_b.at[p, span], recv_b.at[p, span], sem("b_send"), sem("b", g, p), tensor=flip(ten, (q + p) % bits)
            ).start()

    def exchange_f(p):
        for q in range(2):
            span = pl.ds(q * (rows // 2), rows // 2)
            remote(
                send_f.at[p, span], recv_f.at[p, span], sem("f_send"), sem("f", p), tensor=flip(ten, (q + p) % bits)
            ).start()

    def arrived(target, recv):
        remote(target, target, sem("b_send"), recv, tensor=flip(ten, 0)).wait_recv()

    def squares(p):
        return remote(sq_out.at[p], sq_in.at[p], sem("sq", "s", p), sem("sq", "r", p), tensor=flip(ten, p))

    eye = lax.broadcasted_iota(jnp.int32, (rows, rows), 0) == lax.broadcasted_iota(jnp.int32, (rows, rows), 1)

    def to_row(column):
        return jnp.sum(jnp.where(eye, column, 0.0), axis=0, keepdims=True)

    def to_column(row):
        return jnp.sum(jnp.where(eye, row, 0.0), axis=1, keepdims=True)

    def spread(column, count):
        lane = lax.broadcasted_iota(jnp.int32, (column.shape[0], padded - rank), 1)
        result = jnp.zeros(lane.shape, F32)
        for i in range(count):
            piece = column.astype(BF16).astype(F32)
            result = jnp.where(lane == i, piece, result)
            column = column - piece
        return result.astype(BF16)

    for name in ("gain", "sav", "down"):
        loads[name].wait()
    square_s = jnp.zeros((rows, 1), F32)
    total_s = jnp.zeros((rows, rank), F32)
    for cols in columns:
        values = sav[:, cols].astype(F32)
        square_s += jnp.sum(values * values, axis=1, keepdims=True)
        gained = (values * gain[:, cols].astype(F32)).astype(BF16)
        scaled[:, cols] = gained
        total_s += contract_last(gained, down[:, cols])
    square_row = to_row(square_s)
    if bits:
        sq_out[0] = square_row
    for name in ("len", "grad", "up", "fwd"):
        loads[name].wait()

    pl.semaphore_wait(barrier, bits + n_dp - 1 + jnp.where(sec > 0, 1, 0) + jnp.where(sec < n_sec - 1, 1, 0))

    @pl.when(sec > 0)
    def _():
        for copy in (raw_savs, raw_downs, raw_gains):
            copy.start()

    @pl.when(sec < n_sec - 1)
    def _():
        for copy in (raw_ups, raw_fwds):
            copy.start()

    position = lax.broadcasted_iota(jnp.int32, (rows, 1), 0)
    seq_rows = rows // n_seq
    limit = jnp.full((rows, 1), 0, jnp.int32)
    for i in range(n_seq):
        limit = jnp.where(position >= i * seq_rows, i * seq_rows + lens[0, i], limit)
    keep = position < limit
    total_g = jnp.zeros((rows, rank), F32)
    for cols in columns[::-1]:
        held = jnp.where(keep, kept[:, cols].astype(F32), 0.0).astype(BF16)
        kept[:, cols] = held
        total_g += contract_last(held, up[:, cols])
    total_b = jnp.concatenate([total_g, total_s], axis=1)
    acc_b[...] = total_b
    if bits:
        send_b[0] = total_b.astype(BF16)
    if bits:
        for g, (start, size) in enumerate(groups):
            exchange_b(start, size, g, 0)
            if g == 0:
                squares(0).start()

    @pl.when(sec > 0)
    def _():
        raw_keeps.start()

    total = jnp.zeros((rows, rank), F32)
    square_f = jnp.zeros((rows, 1), F32)
    for cols in columns:
        values = fwd[:, cols].astype(F32)
        square_f += jnp.sum(values * values, axis=1, keepdims=True)
        gained = (values * gain[:, cols].astype(F32)).astype(BF16)
        total += contract_last(gained, down[:, cols])

    def begin_f(p):
        send_f[p, :, :rank] = total.astype(BF16)
        send_f[p, :, rank:] = spread(square_f, 3)
        exchange_f(p)

    if bits:
        begin_f(0)
    for p in range(1, bits):
        squares(p - 1).wait_recv()
        square_row += sq_in[p - 1]
        sq_out[p] = square_row
        squares(p).start()
        for g, (start, size) in enumerate(groups):
            span = pl.ds(start, size)
            arrived(recv_b.at[p - 1, span], sem("b", g, p - 1))
            summed = acc_b[span] + recv_b[p - 1, span].astype(F32)
            acc_b[span] = summed
            send_b[p, span] = summed.astype(BF16)
            exchange_b(start, size, g, p)
        arrived(recv_f.at[p - 1], sem("f", p - 1))
        total += recv_f[p - 1, :, :rank].astype(F32)
        square_f += jnp.sum(recv_f[p - 1, :, rank:].astype(F32), axis=1, keepdims=True)
        begin_f(p)

    done_f = [slice(a, min(a + chunk, width - raw_f)) for a in range(0, width - raw_f, chunk)]
    done_b = [slice(a, min(a + chunk, width - raw_b)) for a in range(0, width - raw_b, chunk)]

    def shift(way, start, size, cols):
        source, target = ((out_f, next_in), (out_b, next_gr))[way]
        part_rows, span = pl.ds(start, size), pl.ds(cols.start, cols.stop - cols.start)
        name = ("out_f", "out_b")[way]
        return across(
            1 - 2 * way, source.at[part_rows, span], target.at[part_rows, span], sem(name, "s"), sem(name, "r")
        )

    if bits:
        squares(bits - 1).wait_recv()
        square_row += sq_in[bits - 1]
    scale_s = lax.rsqrt(to_column(square_row) / full_width + EPSILON)
    acts_s, backs_s, tilts = [], [], []

    def give_back(start, size, back_rows, tilt):
        span = slice(start, start + size)
        for cols in done_b:
            normed = jnp.dot(back_rows, down[:, cols], preferred_element_type=F32)
            out_b[span, cols] = (
                kept[span, cols].astype(F32)
                + gain[:, cols].astype(F32) * normed
                - sav[span, cols].astype(F32) * tilt
            ).astype(BF16)
            shift(1, start, size, cols).start()

    for g, (start, size) in enumerate(groups):
        span = slice(start, start + size)
        if bits:
            arrived(recv_b.at[bits - 1, pl.ds(start, size)], sem("b", g, bits - 1))
            summed = acc_b[span] + recv_b[bits - 1, span].astype(F32)
        else:
            summed = acc_b[span]
        own_scale = scale_s[span]
        slope = summed[:, :rank]
        rank_s = summed[:, rank:] * own_scale
        gate = jax.nn.sigmoid(rank_s)
        acts_s.append((rank_s * gate).astype(BF16))
        back = slope * (gate * (1.0 + rank_s * (1.0 - gate)))
        tilts.append(jnp.sum(back.astype(BF16).astype(F32) * rank_s, axis=1, keepdims=True) * (own_scale * own_scale / full_width))
        backs_s.append((back * own_scale).astype(BF16))
        if g == 0 and len(groups) > 1:
            @pl.when(sec > 0)
            def _():
                give_back(start, size, backs_s[0], tilts[0])

    early = 1 if len(groups) > 1 else 0

    @pl.when(sec > 0)
    def _():
        for (start, size), back_rows, tilt in zip(groups, backs_s, tilts):
            back_out[start:start + size, :rank] = back_rows
            back_out[start:start + size, rank:] = spread(tilt, 2)
        backs.start()
        for (start, size), back_rows, tilt in list(zip(groups, backs_s, tilts))[early:]:
            give_back(start, size, back_rows, tilt)

    back_scaled = jnp.concatenate(backs_s, axis=0)
    act_s = jnp.concatenate(acts_s, axis=0)

    if bits:
        arrived(recv_f.at[bits - 1], sem("f", bits - 1))
        total += recv_f[bits - 1, :, :rank].astype(F32)
        square_f += jnp.sum(recv_f[bits - 1, :, rank:].astype(F32), axis=1, keepdims=True)
    rank_f = total * lax.rsqrt(square_f / full_width + EPSILON)
    act_f = (rank_f * jax.nn.sigmoid(rank_f)).astype(BF16)

    @pl.when(sec < n_sec - 1)
    def _():
        act_out[:, :rank] = act_f
        act_out[:, rank:] = jnp.zeros((rows, padded - rank), BF16)
        acts.start()
        for cols in done_f:
            grown = jnp.dot(act_f, up[:, cols], preferred_element_type=F32)
            out_f[:, cols] = (fwd[:, cols].astype(F32) + grown).astype(BF16)
            shift(0, 0, rows, cols).start()

    @pl.when(sec > 0)
    def _():
        raw_ups.wait_recv()
        for k in range(1, n_dp):
            relay(0, k).start()

    @pl.when(sec < n_sec - 1)
    def _():
        raw_downs.wait_recv()
        for k in range(1, n_dp):
            relay(1, k).start()

    def trade(k):
        target = (dp + k) % n_dp
        return remote(
            part.at[:, pl.ds(pl.multiple_of(target * share, share), share)], part_recv.at[k - 1],
            sem("trade", "s", k), sem("trade", "r", k), dp=target,
        )

    for i, (left_side, right_side) in enumerate(((back_scaled, scaled), (act_s, kept))):
        for cols in columns:
            part[i, :, cols] = contract_rows(left_side, right_side[:, cols]).astype(BF16)
    for k in range(1, n_dp):
        trade(k).start()

    @pl.when(sec == 0)
    def _():
        next_in[...] = jnp.zeros_like(next_in)

    @pl.when(sec == n_sec - 1)
    def _():
        next_gr[...] = jnp.zeros_like(next_gr)

    def gather(p):
        held_rows = quarter << p
        block = pl.ds(pl.multiple_of(ten // (1 << p) * held_rows, held_rows), held_rows)
        return remote(pair.at[block], pair.at[block], sem("all", "s", p), sem("all", "r", p), tensor=flip(ten, p))

    @pl.when(sec > 0)
    def _():
        acts.wait_recv()

    @pl.when(sec < n_sec - 1)
    def _():
        backs.wait_recv()

    if bits:
        gather(0).start()

    for k in range(1, n_dp):
        trade(k).wait()
    for i, out in enumerate((grad_down, grad_up)):
        for cols in columns:
            summed = part[i, mine, cols].astype(F32)
            for k in range(1, n_dp):
                summed += part_recv[k - 1, i, :, cols].astype(F32)
            out[:, cols] = (summed * (1.0 / n_dp)).astype(BF16)

    for p in range(bits):
        gather(p).wait()
        if p + 1 < bits:
            gather(p + 1).start()

    @pl.when(sec > 0)
    def _():
        for k in range(1, n_dp):
            relay(0, k).wait()
        raw_fwds.wait_recv()
        for a in range(0, raw_f, chunk):
            b = min(a + chunk, raw_f)
            grown = jnp.dot(pair[:, :rank], raw_up[:, a:b], preferred_element_type=F32)
            next_in[:, width - raw_f + a:width - raw_f + b] = (raw_fwd[:, a:b].astype(F32) + grown).astype(BF16)

    @pl.when(sec < n_sec - 1)
    def _():
        for k in range(1, n_dp):
            relay(1, k).wait()
        raw_gains.wait_recv()
        raw_pairs.wait_recv()
        far_tilt = jnp.sum(pair[:, padded + rank:].astype(F32), axis=1, keepdims=True)
        for a in range(0, raw_b, chunk):
            b = min(a + chunk, raw_b)
            normed = jnp.dot(pair[:, padded:padded + rank], raw_down[:, a:b], preferred_element_type=F32)
            next_gr[:, width - raw_b + a:width - raw_b + b] = (
                raw_pair[1, :, a:b].astype(F32)
                + raw_gain[:, a:b].astype(F32) * normed
                - raw_pair[0, :, a:b].astype(F32) * far_tilt
            ).astype(BF16)

    if bits:
        for p in range(bits):
            squares(p).wait_send()
        remote(send_b, recv_b, sem("b_send"), sem("b", 0, 0), tensor=flip(ten, 0)).wait_send()
        remote(send_f, recv_f, sem("f_send"), sem("f", 0), tensor=flip(ten, 0)).wait_send()

    whole_f = across(1, fwd, out_f, sem("out_f", "s"), sem("out_f", "r"))
    whole_b = across(-1, kept, out_b, sem("out_b", "s"), sem("out_b", "r"))

    @pl.when(sec < n_sec - 1)
    def _():
        for copy in (raw_ups, acts, whole_f):
            copy.wait_send()

    @pl.when(sec > 0)
    def _():
        for copy in (raw_savs, raw_downs, raw_gains, backs, whole_b):
            copy.wait_send()

    @pl.when(sec < n_sec - 1)
    def _():
        shift(1, 0, rows, slice(0, width - raw_b)).wait_recv()

    @pl.when(sec > 0)
    def _():
        shift(0, 0, rows, slice(0, width - raw_f)).wait_recv()


def place(*refs):
    count = len(refs) // 2
    sems = refs[-1]
    copies = [pltpu.make_async_copy(refs[i], refs[count + i], sems.at[i]) for i in range(count)]
    for copy in copies:
        copy.start()
    for copy in copies:
        copy.wait()


def solution(mesh):
    n_sec, n_ten, n_dp = (mesh.shape[name] for name in ("section", "tensor", "dp"))

    def shards(forward_rows, saved_rows, output_grad, lengths, norm_gain, down_map, up_map):
        rows, width = forward_rows.shape[2:]
        rank = down_map.shape[1]
        n_seq = lengths.shape[2]
        share = rank // n_dp
        bits = n_ten.bit_length() - 1
        chunk = min(width, 4 * LANES)
        raw_f = int(width * RAW_FORWARD) // LANES * LANES
        raw_b = int(width * RAW_BACK) // LANES * LANES
        steps = max(bits, 1)
        padded = (rank + 3 + LANES - 1) // LANES * LANES
        vmem = pl.BlockSpec(memory_space=pltpu.VMEM)
        anywhere = pl.BlockSpec(memory_space=pl.ANY)
        flops = 7 * 2 * rows * rank * width
        dma = pltpu.SemaphoreType.DMA
        shapes = ((rows, width),) * 2 + ((share, width),) * 2
        results = pl.pallas_call(
            functools.partial(tick, (n_sec, n_ten, n_dp, chunk)),
            out_shape=tuple(pltpu.VMEM(shape, BF16) for shape in shapes),
            in_specs=[anywhere] * 7,
            out_specs=(vmem,) * 4,
            scratch_shapes=[
                pltpu.SMEM((1, n_seq), jnp.int32),
                pltpu.VMEM((1, width), BF16),
                pltpu.VMEM((rows, width), BF16),
                pltpu.VMEM((rows, width), BF16),
                pltpu.VMEM((rows, width), BF16),
                pltpu.VMEM((rank, width), BF16),
                pltpu.VMEM((rank, width), BF16),
                pltpu.VMEM((rows, width), BF16),
                pltpu.VMEM((rows, padded), F32),
                pltpu.VMEM((rows, 2 * rank), F32),
                pltpu.VMEM((steps, rows, padded), BF16),
                pltpu.VMEM((steps, rows, padded), BF16),
                pltpu.VMEM((steps, rows, 2 * rank), BF16),
                pltpu.VMEM((steps, rows, 2 * rank), BF16),
                pltpu.VMEM((rows, width), BF16),
                pltpu.VMEM((rows, width), BF16),
                pltpu.VMEM((2, rank, width), BF16),
                pltpu.VMEM((max(n_dp - 1, 1), 2, share, width), BF16),
                pltpu.VMEM((rows, padded), BF16),
                pltpu.VMEM((rows, padded), BF16),
                pltpu.VMEM((rows, 2 * padded), BF16),
                pltpu.VMEM((steps, 1, rows), F32),
                pltpu.VMEM((steps, 1, rows), F32),
                pltpu.VMEM((rows, raw_f), BF16),
                pltpu.VMEM((rank, raw_f), BF16),
                pltpu.VMEM((2, rows, raw_b), BF16),
                pltpu.VMEM((rank, raw_b), BF16),
                pltpu.VMEM((1, raw_b), BF16),
                dma((len(semaphores(len(row_groups(rows)), bits, n_dp)),)),
            ],
            compiler_params=pltpu.CompilerParams(collective_id=0, has_side_effects=True),
            cost_estimate=pl.CostEstimate(
                flops=flops, bytes_accessed=16 * rows * width, transcendentals=4 * rows * rank
            ),
            name="tick",
        )(
            forward_rows[0, 0], saved_rows[0, 0], output_grad[0, 0], lengths[0], norm_gain, down_map[0], up_map[0]
        )
        next_inputs, next_grads, grad_down, grad_up = pl.pallas_call(
            place,
            out_shape=tuple(jax.ShapeDtypeStruct(shape, BF16) for shape in shapes),
            in_specs=[vmem] * 4,
            out_specs=(anywhere,) * 4,
            scratch_shapes=[dma((4,))],
            name="place",
        )(*[pltpu.with_memory_space_constraint(x, pltpu.VMEM) for x in results])
        return next_inputs[None, None], next_grads[None, None], grad_down[None], grad_up[None]

    row_spec = P("section", "dp", None, "tensor")
    map_spec = P("section", None, "tensor")
    part_spec = P("section", "dp", "tensor")
    return jax.shard_map(
        shards,
        mesh=mesh,
        in_specs=(row_spec, row_spec, row_spec, P("section", "dp"), P("section", "tensor"), map_spec, map_spec),
        out_specs=(row_spec, row_spec, part_spec, part_spec),
        check_vma=False,
    )
```

time: 33.2 us -> 29.9 us (0.901)
  Pallas kernels: 32.3 us -> 29.1 us
    pallas_call x1, Pallas kernels: 30.9 us -> 27.7 us  [shards(): pl.pallas_call(functools.partial(tick, (n_sec, n_ten, n_dp, chunk)), out_...]
where the time goes in v1:
time: 29.9 us; the launch traced here: 29.8 us
  Pallas kernels  29.1 us (97%)
  between operations  0.64 us (2%)
    pallas_call x1, Pallas kernels, shards(): pl.pallas_call(functools.partial(tick, (n_sec, n_ten, n_dp, chunk)), out_...  27.7 us
    pallas_call x1, Pallas kernels, shards(): pl.pallas_call(place, out_shape=tuple((jax.ShapeDtypeStruct(shape, BF16)...  1.43 us

profile of v1, /device:TPU:0, one launch (start us, length us, event | category | flops | bytes accessed | tf_op | source)
XLA Modules:
  0.0 29.8 jit_solution(3870274747146869847)
XLA Ops:
  0.6 27.7 %tick.1 = (bf16[192,2048]{1,0:T(8,128)(2,1)S(1)}, bf16[192,2048]{1,0:T(8,128)(2,1)S(1)}, bf16[96,2048]{1,0:T(8,128)(2,1)S(1)}, bf16[96,2048]{1,0:T(8,128)(2,1)S(1)}) custom-call(bf16[192,2048]{1,0:T(8,128)(2,1)} %bitcast.10, bf16[192,2048]{1,0:T(8,128)(2,1)} %bitcast.11, bf16[192,2048]{1,0:T(8,128)(2,1)} %bitcast.12, s32[1,2]{1,0:T(1,128)} %bitcast.15, ...), custom_call_target="tpu_custom_call" | custom-call | flops 1056964608 | bytes 6291456 | tf_op jit(solution)/shard_map/tick/pallas_call | solution.py:484
  28.3 1.4 %place.1 = (bf16[192,2048]{1,0:T(8,128)(2,1)}, bf16[192,2048]{1,0:T(8,128)(2,1)}, bf16[96,2048]{1,0:T(8,128)(2,1)}, bf16[96,2048]{1,0:T(8,128)(2,1)}) custom-call(bf16[192,2048]{1,0:T(8,128)(2,1)S(1)} %get-tuple-element.12.refs_0_, bf16[192,2048]{1,0:T(8,128)(2,1)S(1)} %get-tuple-element.13.refs_1_, bf16[96,2048]{1,0:T(8,128)(2,1)S(1)} %get-tuple-element.14.refs_2_, ...), custom_call_target="tpu_custom_call" | custom-call | tf_op jit(solution)/shard_map/place/pallas_call | solution.py:528

commit v2 on v1

--- a/solution.py
+++ b/solution.py
@@ -32,6 +32,13 @@
     return index + step * (1 - 2 * ((index // step) % 2))
 
 
+def peer(index, k, bits):
+    for bit in range(bits):
+        if k >> bit & 1:
+            index = flip(index, bit)
+    return index
+
+
 def row_groups(rows):
     sizes = (rows // 6, rows // 3, rows // 2) if rows % 192 == 0 else (rows,)
     starts = [sum(sizes[:i]) for i in range(len(sizes))]
@@ -39,12 +46,12 @@
 
 
 def semaphores(n_group, bits, n_dp):
-    names = ["len", "gain", "sav", "down", "grad", "up", "fwd"]
-    names += [("sq", kind, p) for kind in "sr" for p in range(bits)]
-    names += [("b", g, p) for g in range(n_group) for p in range(bits)] + ["b_send"]
+    names = ["len", "gain", "fwd", "sav_tail", "sav", "down", "kept_up"]
+    names += [(side, kind) for side in ("sq", "first") for kind in "sr"]
+    names += [("b", g, p) for g in range(1, n_group) for p in range(bits)] + ["b_send"]
     names += [("f", p) for p in range(bits)] + ["f_send"]
     names += [(side, kind) for side in ("out_f", "out_b") for kind in "sr"]
-    names += [(side, kind) for side in ("raw_up", "raw_down", "raw_gain", "act", "back") for kind in "sr"]
+    names += [(side, kind) for side in ("raw_up", "raw_down", "act", "back") for kind in "sr"]
     names += ["raw_fwd_r", "raw_sav_s", "raw_pair_r"]
     names += [("all", kind, p) for kind in "sr" for p in range(bits)]
     names += [("trade", kind, k) for kind in "sr" for k in range(1, n_dp)]
@@ -54,13 +61,15 @@
 
 def tick(sizes, fwd_hbm, sav_hbm, grad_hbm, len_hbm, gain_hbm, down_hbm, up_hbm,
          next_in, next_gr, grad_down, grad_up,
-         lens, gain, fwd, sav, kept, down, up, scaled,
-         acc_f, acc_b, send_f, recv_f, send_b, recv_b, out_f, out_b,
+         lens, gain, fwd, sav_down, kept_up, gained,
+         acc_b, send_f, recv_f, send_b, recv_b, first_b, out_f, out_b,
          part, part_recv, act_out, back_out, pair, sq_out, sq_in,
-         raw_fwd, raw_up, raw_pair, raw_down, raw_gain, sems):
+         raw_fwd, raw_up, raw_pair, raw_down, sems, far_sem):
     n_sec, n_ten, n_dp, chunk = sizes
     rows, width = fwd.shape
-    rank = down.shape[0]
+    rank = down_hbm.shape[0]
+    sav, down = sav_down.at[pl.ds(0, rows)], sav_down.at[pl.ds(rows, rank)]
+    kept, up = kept_up.at[pl.ds(0, rows)], kept_up.at[pl.ds(rows, rank)]
     padded = act_out.shape[1]
     full_width = width * n_ten
     n_seq = lens.shape[1]
@@ -68,22 +77,13 @@
     share = rank // n_dp
     quarter = rows // n_ten
     groups = row_groups(rows)
+    columns = [slice(c, c + chunk) for c in range(0, width, chunk)]
     index = semaphores(len(groups), bits, n_dp)
     sec, ten, dp = lax.axis_index("section"), lax.axis_index("tensor"), lax.axis_index("dp")
 
     def sem(*name):
         return sems.at[index[name if len(name) > 1 else name[0]]]
 
-    loads = {
-        name: pltpu.make_async_copy(source, target, sem(name))
-        for name, source, target in (
-            ("sav", sav_hbm, sav), ("gain", gain_hbm, gain), ("down", down_hbm, down), ("len", len_hbm, lens),
-            ("grad", grad_hbm, kept), ("up", up_hbm, up), ("fwd", fwd_hbm, fwd),
-        )
-    }
-    for load in loads.values():
-        load.start()
-
     @pl.when(sec == 0)
     def _():
         pair[:, :padded] = jnp.zeros((rows, padded), BF16)
@@ -93,8 +93,10 @@
         pair[:, padded:] = jnp.zeros((rows, padded), BF16)
 
     barrier = pltpu.get_barrier_semaphore()
-    for p in range(bits):
-        pl.semaphore_signal(barrier, inc=1, device_id={"tensor": flip(ten, p)})
+    relayed = bits == 2
+    near = [1 << bit for bit in range(bits)] if relayed else range(1, n_ten)
+    for k in near:
+        pl.semaphore_signal(barrier, inc=1, device_id={"tensor": peer(ten, k, bits)})
     for k in range(1, n_dp):
         pl.semaphore_signal(barrier, inc=1, device_id={"dp": (dp + k) % n_dp})
 
@@ -106,11 +108,30 @@
     def _():
         pl.semaphore_signal(barrier, inc=1, device_id={"section": sec + 1})
 
-    columns = [slice(c, c + chunk) for c in range(0, width, chunk)]
     raw_f, raw_b = raw_fwd.shape[1], raw_pair.shape[2]
     mine = pl.ds(pl.multiple_of(dp * share, share), share)
     own = pl.ds(pl.multiple_of(ten * quarter, quarter), quarter)
     tail_f, tail_b = pl.ds(width - raw_f, raw_f), pl.ds(width - raw_b, raw_b)
+    loads = {
+        name: pltpu.make_async_copy(source, target, sem(name))
+        for name, source, target in (
+            ("gain", gain_hbm, gain), ("len", len_hbm, lens), ("fwd", fwd_hbm, fwd),
+            ("sav_tail", sav_hbm.at[:, tail_b], sav.at[:, tail_b]),
+            ("sav", sav_hbm.at[:, pl.ds(0, width - raw_b)], sav.at[:, pl.ds(0, width - raw_b)]),
+            ("down", down_hbm, down),
+        )
+    }
+    loads["sav_tail"].start()
+    loads["gain"].start()
+    loads["sav"].start()
+    loads["down"].start()
+    for name, both, sources in (("kept_up", kept_up, (grad_hbm, up_hbm)),):
+        loads[name] = pltpu.make_async_copy(both, both, sem(name))
+        for source, first in zip(sources, (0, rows)):
+            pltpu.make_async_copy(source, both.at[pl.ds(first, source.shape[0])], sem(name)).start()
+    loads["len"].start()
+    loads["fwd"].start()
+
 
     def remote(source, target, send, recv, **place):
         return pltpu.make_async_remote_copy(
@@ -123,8 +144,7 @@
     raw_ups = across(1, up.at[mine, tail_f], raw_up.at[mine], sem("raw_up", "s"), sem("raw_up", "r"))
     raw_fwds = across(1, fwd.at[:, tail_f], raw_fwd, sem("out_f", "s"), sem("raw_fwd_r"))
     acts = across(1, act_out.at[own], pair.at[own, pl.ds(0, padded)], sem("act", "s"), sem("act", "r"))
-    raw_downs = across(-1, down.at[mine, tail_b], raw_down.at[mine], sem("raw_down", "s"), sem("raw_down", "r"))
-    raw_gains = across(-1, gain.at[:, tail_b], raw_gain, sem("raw_gain", "s"), sem("raw_gain", "r"))
+    raw_downs = across(-1, gained.at[mine, tail_b], raw_down.at[mine], sem("raw_down", "s"), sem("raw_down", "r"))
     raw_savs = across(-1, sav.at[:, tail_b], raw_pair.at[0], sem("raw_sav_s"), sem("raw_pair_r"))
     raw_keeps = across(-1, kept.at[:, tail_b], raw_pair.at[1], sem("out_b", "s"), sem("raw_pair_r"))
     raw_pairs = across(-1, raw_pair, raw_pair, sem("raw_sav_s"), sem("raw_pair_r"))
@@ -133,6 +153,16 @@
     def relay(way, k):
         ref = (raw_up, raw_down)[way].at[mine]
         return remote(ref, ref, sem("relay", way, "s", k), sem("relay", way, "r", k), dp=(dp + k) % n_dp)
+
+    first_rows = groups[0][1]
+
+    def exchange_first():
+        for k in range(n_ten - 1, 0, -1):
+            place = {"tensor": peer(ten, k, bits)}
+            remote(
+                send_b.at[0, pl.ds(0, first_rows)], first_b.at[k - 1], sem("first", "s"), sem("first", "r"), **place
+            ).start()
+            remote(sq_out, sq_in.at[k - 1], sem("sq", "s"), sem("sq", "r"), **place).start()
 
     def exchange_b(start, size, g, p):
         for q in range(2):
@@ -149,10 +179,7 @@
             ).start()
 
     def arrived(target, recv):
-        remote(target, target, sem("b_send"), recv, tensor=flip(ten, 0)).wait_recv()
-
-    def squares(p):
-        return remote(sq_out.at[p], sq_in.at[p], sem("sq", "s", p), sem("sq", "r", p), tensor=flip(ten, p))
+        remote(target, target, sem("f_send"), recv, tensor=flip(ten, 0)).wait_recv()
 
     eye = lax.broadcasted_iota(jnp.int32, (rows, rows), 0) == lax.broadcasted_iota(jnp.int32, (rows, rows), 1)
 
@@ -171,6 +198,16 @@
             column = column - piece
         return result.astype(BF16)
 
+    loads["sav_tail"].wait()
+
+    pl.semaphore_wait(barrier, len(near) + n_dp - 1 + jnp.where(sec > 0, 1, 0) + jnp.where(sec < n_sec - 1, 1, 0))
+    if relayed:
+        pl.semaphore_signal(far_sem, inc=1, device_id={"tensor": flip(ten, 0)})
+
+    @pl.when(sec > 0)
+    def _():
+        raw_savs.start()
+
     for name in ("gain", "sav", "down"):
         loads[name].wait()
     square_s = jnp.zeros((rows, 1), F32)
@@ -178,26 +215,23 @@
     for cols in columns:
         values = sav[:, cols].astype(F32)
         square_s += jnp.sum(values * values, axis=1, keepdims=True)
-        gained = (values * gain[:, cols].astype(F32)).astype(BF16)
-        scaled[:, cols] = gained
-        total_s += contract_last(gained, down[:, cols])
+        scaled = down[:, cols] * gain[:, cols]
+        gained[:, cols] = scaled
+        total_s += contract_last(sav[:, cols], scaled)
     square_row = to_row(square_s)
     if bits:
-        sq_out[0] = square_row
-    for name in ("len", "grad", "up", "fwd"):
-        loads[name].wait()
-
-    pl.semaphore_wait(barrier, bits + n_dp - 1 + jnp.where(sec > 0, 1, 0) + jnp.where(sec < n_sec - 1, 1, 0))
-
-    @pl.when(sec > 0)
-    def _():
-        for copy in (raw_savs, raw_downs, raw_gains):
-            copy.start()
-
-    @pl.when(sec < n_sec - 1)
-    def _():
-        for copy in (raw_ups, raw_fwds):
-            copy.start()
+        sq_out[...] = square_row
+
+    @pl.when(sec > 0)
+    def _():
+        raw_downs.start()
+
+    loads["len"].wait()
+    loads["kept_up"].wait()
+
+    @pl.when(sec < n_sec - 1)
+    def _():
+        raw_ups.start()
 
     position = lax.broadcasted_iota(jnp.int32, (rows, 1), 0)
     seq_rows = rows // n_seq
@@ -206,19 +240,26 @@
         limit = jnp.where(position >= i * seq_rows, i * seq_rows + lens[0, i], limit)
     keep = position < limit
     total_g = jnp.zeros((rows, rank), F32)
-    for cols in columns[::-1]:
-        held = jnp.where(keep, kept[:, cols].astype(F32), 0.0).astype(BF16)
-        kept[:, cols] = held
-        total_g += contract_last(held, up[:, cols])
-    total_b = jnp.concatenate([total_g, total_s], axis=1)
+    for cols in columns:
+        total_g += contract_last(kept[:, cols], up[:, cols])
+    total_b = jnp.concatenate([jnp.where(keep, total_g, 0.0), total_s], axis=1)
     acc_b[...] = total_b
     if bits:
         send_b[0] = total_b.astype(BF16)
-    if bits:
-        for g, (start, size) in enumerate(groups):
+        if relayed:
+            pl.semaphore_wait(far_sem, 1)
+        exchange_first()
+        for g, (start, size) in list(enumerate(groups))[1:]:
             exchange_b(start, size, g, 0)
-            if g == 0:
-                squares(0).start()
+
+    loads["fwd"].wait()
+
+    @pl.when(sec < n_sec - 1)
+    def _():
+        raw_fwds.start()
+
+    for cols in columns[::-1]:
+        kept[:, cols] = jnp.where(keep, kept[:, cols].astype(F32), 0.0).astype(BF16)
 
     @pl.when(sec > 0)
     def _():
@@ -229,32 +270,27 @@
     for cols in columns:
         values = fwd[:, cols].astype(F32)
         square_f += jnp.sum(values * values, axis=1, keepdims=True)
-        gained = (values * gain[:, cols].astype(F32)).astype(BF16)
-        total += contract_last(gained, down[:, cols])
-
-    def begin_f(p):
+        total += contract_last(fwd[:, cols], gained[:, cols])
+
+    def begin_f(p, total, square_f):
         send_f[p, :, :rank] = total.astype(BF16)
         send_f[p, :, rank:] = spread(square_f, 3)
         exchange_f(p)
 
     if bits:
-        begin_f(0)
-    for p in range(1, bits):
-        squares(p - 1).wait_recv()
-        square_row += sq_in[p - 1]
-        sq_out[p] = square_row
-        squares(p).start()
-        for g, (start, size) in enumerate(groups):
+        begin_f(0, total, square_f)
+    def step_b(p, chosen):
+        for g, (start, size) in chosen:
             span = pl.ds(start, size)
             arrived(recv_b.at[p - 1, span], sem("b", g, p - 1))
             summed = acc_b[span] + recv_b[p - 1, span].astype(F32)
             acc_b[span] = summed
             send_b[p, span] = summed.astype(BF16)
             exchange_b(start, size, g, p)
-        arrived(recv_f.at[p - 1], sem("f", p - 1))
-        total += recv_f[p - 1, :, :rank].astype(F32)
-        square_f += jnp.sum(recv_f[p - 1, :, rank:].astype(F32), axis=1, keepdims=True)
-        begin_f(p)
+
+    later = list(enumerate(groups))[1:]
+    if bits > 1:
+        step_b(1, later[:1])
 
     done_f = [slice(a, min(a + chunk, width - raw_f)) for a in range(0, width - raw_f, chunk)]
     done_b = [slice(a, min(a + chunk, width - raw_b)) for a in range(0, width - raw_b, chunk)]
@@ -268,25 +304,37 @@
         )
 
     if bits:
-        squares(bits - 1).wait_recv()
-        square_row += sq_in[bits - 1]
+        arrived(sq_in, sem("sq", "r"))
+        for k in range(1, n_ten):
+            square_row += sq_in[k - 1]
     scale_s = lax.rsqrt(to_column(square_row) / full_width + EPSILON)
     acts_s, backs_s, tilts = [], [], []
 
-    def give_back(start, size, back_rows, tilt):
+    def give_back(start, size, back_rows, tilt, first):
         span = slice(start, start + size)
         for cols in done_b:
-            normed = jnp.dot(back_rows, down[:, cols], preferred_element_type=F32)
+            normed = jnp.dot(back_rows, gained[:, cols], preferred_element_type=F32)
             out_b[span, cols] = (
                 kept[span, cols].astype(F32)
-                + gain[:, cols].astype(F32) * normed
+                + normed
                 - sav[span, cols].astype(F32) * tilt
             ).astype(BF16)
+            if first or cols in done_b[:1]:
+                shift(1, start, size, cols).start()
+
+    def send_late():
+        start, size = groups[-1]
+        for cols in done_b[1:]:
             shift(1, start, size, cols).start()
 
     for g, (start, size) in enumerate(groups):
         span = slice(start, start + size)
-        if bits:
+        if bits and g == 0:
+            arrived(first_b, sem("first", "r"))
+            summed = acc_b[span]
+            for k in range(1, n_ten):
+                summed += first_b[k - 1].astype(F32)
+        elif bits:
             arrived(recv_b.at[bits - 1, pl.ds(start, size)], sem("b", g, bits - 1))
             summed = acc_b[span] + recv_b[bits - 1, span].astype(F32)
         else:
@@ -302,7 +350,19 @@
         if g == 0 and len(groups) > 1:
             @pl.when(sec > 0)
             def _():
-                give_back(start, size, backs_s[0], tilts[0])
+                give_back(start, size, backs_s[0], tilts[0], True)
+        if 0 < g < len(groups) - 1:
+            @pl.when(jnp.logical_and(sec > 0, dp % 2 == 1))
+            def _():
+                give_back(start, size, backs_s[g], tilts[g], True)
+        if g == 0:
+            for p in range(1, bits):
+                step_b(p, later[1:] if p == 1 else later)
+            for p in range(1, bits):
+                arrived(recv_f.at[p - 1], sem("f", p - 1))
+                total += recv_f[p - 1, :, :rank].astype(F32)
+                square_f += jnp.sum(recv_f[p - 1, :, rank:].astype(F32), axis=1, keepdims=True)
+                begin_f(p, total, square_f)
 
     early = 1 if len(groups) > 1 else 0
 
@@ -312,8 +372,12 @@
             back_out[start:start + size, :rank] = back_rows
             back_out[start:start + size, rank:] = spread(tilt, 2)
         backs.start()
-        for (start, size), back_rows, tilt in list(zip(groups, backs_s, tilts))[early:]:
-            give_back(start, size, back_rows, tilt)
+        for g in range(early, len(groups) - 1):
+            @pl.when(dp % 2 == 0)
+            def _():
+                give_back(*groups[g], backs_s[g], tilts[g], True)
+        give_back(*groups[-1], backs_s[-1], tilts[-1], False)
+        pl.when(dp % 2 == 0)(send_late)
 
     back_scaled = jnp.concatenate(backs_s, axis=0)
     act_s = jnp.concatenate(acts_s, axis=0)
@@ -354,9 +418,9 @@
             sem("trade", "s", k), sem("trade", "r", k), dp=target,
         )
 
-    for i, (left_side, right_side) in enumerate(((back_scaled, scaled), (act_s, kept))):
-        for cols in columns:
-            part[i, :, cols] = contract_rows(left_side, right_side[:, cols]).astype(BF16)
+    for cols in columns:
+        part[0, :, cols] = (contract_rows(back_scaled, sav[:, cols]) * gain[:, cols].astype(F32)).astype(BF16)
+        part[1, :, cols] = contract_rows(act_s, kept[:, cols]).astype(BF16)
     for k in range(1, n_dp):
         trade(k).start()
 
@@ -397,6 +461,8 @@
         gather(p).wait()
         if p + 1 < bits:
             gather(p + 1).start()
+        if p == 0:
+            pl.when(jnp.logical_and(sec > 0, dp % 2 == 1))(send_late)
 
     @pl.when(sec > 0)
     def _():
@@ -412,7 +478,6 @@
     def _():
         for k in range(1, n_dp):
             relay(1, k).wait()
-        raw_gains.wait_recv()
         raw_pairs.wait_recv()
         far_tilt = jnp.sum(pair[:, padded + rank:].astype(F32), axis=1, keepdims=True)
         for a in range(0, raw_b, chunk):
@@ -420,14 +485,16 @@
             normed = jnp.dot(pair[:, padded:padded + rank], raw_down[:, a:b], preferred_element_type=F32)
             next_gr[:, width - raw_b + a:width - raw_b + b] = (
                 raw_pair[1, :, a:b].astype(F32)
-                + raw_gain[:, a:b].astype(F32) * normed
+                + normed
                 - raw_pair[0, :, a:b].astype(F32) * far_tilt
             ).astype(BF16)
 
     if bits:
-        for p in range(bits):
-            squares(p).wait_send()
-        remote(send_b, recv_b, sem("b_send"), sem("b", 0, 0), tensor=flip(ten, 0)).wait_send()
+        remote(sq_in, sq_in, sem("sq", "s"), sem("sq", "r"), tensor=flip(ten, 0)).wait_send()
+        remote(first_b, first_b, sem("first", "s"), sem("first", "r"), tensor=flip(ten, 0)).wait_send()
+        if len(groups) > 1:
+            rest = send_b.at[:, pl.ds(first_rows, rows - first_rows)]
+            remote(rest, rest, sem("b_send"), sem("first", "r"), tensor=flip(ten, 0)).wait_send()
         remote(send_f, recv_f, sem("f_send"), sem("f", 0), tensor=flip(ten, 0)).wait_send()
 
     whole_f = across(1, fwd, out_f, sem("out_f", "s"), sem("out_f", "r"))
@@ -440,7 +507,7 @@
 
     @pl.when(sec > 0)
     def _():
-        for copy in (raw_savs, raw_downs, raw_gains, backs, whole_b):
+        for copy in (raw_savs, raw_downs, backs, whole_b):
             copy.wait_send()
 
     @pl.when(sec < n_sec - 1)
@@ -490,17 +557,15 @@
                 pltpu.SMEM((1, n_seq), jnp.int32),
                 pltpu.VMEM((1, width), BF16),
                 pltpu.VMEM((rows, width), BF16),
+                pltpu.VMEM((rows + rank, width), BF16),
+                pltpu.VMEM((rows + rank, width), BF16),
                 pltpu.VMEM((rows, width), BF16),
-                pltpu.VMEM((rows, width), BF16),
-                pltpu.VMEM((rank, width), BF16),
-                pltpu.VMEM((rank, width), BF16),
-                pltpu.VMEM((rows, width), BF16),
-                pltpu.VMEM((rows, padded), F32),
                 pltpu.VMEM((rows, 2 * rank), F32),
                 pltpu.VMEM((steps, rows, padded), BF16),
                 pltpu.VMEM((steps, rows, padded), BF16),
                 pltpu.VMEM((steps, rows, 2 * rank), BF16),
                 pltpu.VMEM((steps, rows, 2 * rank), BF16),
+                pltpu.VMEM((max(n_ten - 1, 1), row_groups(rows)[0][1], 2 * rank), BF16),
                 pltpu.VMEM((rows, width), BF16),
                 pltpu.VMEM((rows, width), BF16),
                 pltpu.VMEM((2, rank, width), BF16),
@@ -508,14 +573,14 @@
                 pltpu.VMEM((rows, padded), BF16),
                 pltpu.VMEM((rows, padded), BF16),
                 pltpu.VMEM((rows, 2 * padded), BF16),
-                pltpu.VMEM((steps, 1, rows), F32),
-                pltpu.VMEM((steps, 1, rows), F32),
+                pltpu.VMEM((1, rows), F32),
+                pltpu.VMEM((max(n_ten - 1, 1), 1, rows), F32),
                 pltpu.VMEM((rows, raw_f), BF16),
                 pltpu.VMEM((rank, raw_f), BF16),
                 pltpu.VMEM((2, rows, raw_b), BF16),
                 pltpu.VMEM((rank, raw_b), BF16),
-                pltpu.VMEM((1, raw_b), BF16),
                 dma((len(semaphores(len(row_groups(rows)), bits, n_dp)),)),
+                pltpu.SemaphoreType.REGULAR,
             ],
             compiler_params=pltpu.CompilerParams(collective_id=0, has_side_effects=True),
             cost_estimate=pl.CostEstimate(

time: 29.9 us -> 28.4 us (0.950)
  the two profiles are of different devices: /device:TPU:0 before, /device:TPU:1 now
where the time goes in v2:
time: 28.4 us; the launch traced here: 28.2 us
  Pallas kernels  27.6 us (97%)
  between operations  0.64 us (2%)
    pallas_call x1, Pallas kernels, shards(): pl.pallas_call(functools.partial(tick, (n_sec, n_ten, n_dp, chunk)), out_...  26.1 us
    pallas_call x1, Pallas kernels, shards(): pl.pallas_call(place, out_shape=tuple((jax.ShapeDtypeStruct(shape, BF16)...  1.43 us

profile of v2, /device:TPU:1, one launch (start us, length us, event | category | flops | bytes accessed | tf_op | source)
XLA Modules:
  0.0 28.2 jit_solution(12569828112744864207)
XLA Ops:
  0.6 26.1 %tick.1 = (bf16[192,2048]{1,0:T(8,128)(2,1)S(1)}, bf16[192,2048]{1,0:T(8,128)(2,1)S(1)}, bf16[96,2048]{1,0:T(8,128)(2,1)S(1)}, bf16[96,2048]{1,0:T(8,128)(2,1)S(1)}) custom-call(bf16[192,2048]{1,0:T(8,128)(2,1)} %bitcast.10, bf16[192,2048]{1,0:T(8,128)(2,1)} %bitcast.11, bf16[192,2048]{1,0:T(8,128)(2,1)} %bitcast.12, s32[1,2]{1,0:T(1,128)} %bitcast.15, ...), custom_call_target="tpu_custom_call" | custom-call | flops 1056964608 | bytes 6291456 | tf_op jit(solution)/shard_map/tick/pallas_call | solution.py:551
  26.8 1.4 %place.1 = (bf16[192,2048]{1,0:T(8,128)(2,1)}, bf16[192,2048]{1,0:T(8,128)(2,1)}, bf16[96,2048]{1,0:T(8,128)(2,1)}, bf16[96,2048]{1,0:T(8,128)(2,1)}) custom-call(bf16[192,2048]{1,0:T(8,128)(2,1)S(1)} %get-tuple-element.12.refs_0_, bf16[192,2048]{1,0:T(8,128)(2,1)S(1)} %get-tuple-element.13.refs_1_, bf16[96,2048]{1,0:T(8,128)(2,1)S(1)} %get-tuple-element.14.refs_2_, ...), custom_call_target="tpu_custom_call" | custom-call | tf_op jit(solution)/shard_map/place/pallas_call | solution.py:593

commit v3 on v2

--- a/solution.py
+++ b/solution.py
@@ -47,16 +47,21 @@
 
 def semaphores(n_group, bits, n_dp):
     names = ["len", "gain", "fwd", "sav_tail", "sav", "down", "kept_up"]
+    n_load = len(names)
     names += [(side, kind) for side in ("sq", "first") for kind in "sr"]
     names += [("b", g, p) for g in range(1, n_group) for p in range(bits)] + ["b_send"]
     names += [("f", p) for p in range(bits)] + ["f_send"]
     names += [(side, kind) for side in ("out_f", "out_b") for kind in "sr"]
-    names += [(side, kind) for side in ("raw_up", "raw_down", "act", "back") for kind in "sr"]
-    names += ["raw_fwd_r", "raw_sav_s", "raw_pair_r"]
-    names += [("all", kind, p) for kind in "sr" for p in range(bits)]
-    names += [("trade", kind, k) for kind in "sr" for k in range(1, n_dp)]
-    names += [("relay", way, kind, k) for way in range(2) for kind in "sr" for k in range(1, n_dp)]
-    return {name: i for i, name in enumerate(names)}
+    names += [(side, kind) for side in ("raw_up", "raw_down") for kind in "sr"] + [("act", "r"), ("back", "r")]
+    names += ["raw_fwd_r", "raw_sav_s", "raw_pair_r", ("relief", "s"), ("relief", "r")]
+    names += [("all", "r", p) for p in range(bits)] + [("trade", "r", k) for k in range(1, n_dp)]
+    names += [("relay", way, "r", k) for way in range(2) for k in range(1, n_dp)]
+    sends = [("act", "s"), ("back", "s")] + [("all", "s", p) for p in range(bits)]
+    sends += [("trade", "s", k) for k in range(1, n_dp)]
+    sends += [("relay", way, "s", k) for way in range(2) for k in range(1, n_dp)]
+    names += sends[n_load:]
+    index = {name: i for i, name in enumerate(names)}
+    return index | {name: i for i, name in enumerate(sends[:n_load])}
 
 
 def tick(sizes, fwd_hbm, sav_hbm, grad_hbm, len_hbm, gain_hbm, down_hbm, up_hbm,
@@ -64,7 +69,7 @@
          lens, gain, fwd, sav_down, kept_up, gained,
          acc_b, send_f, recv_f, send_b, recv_b, first_b, out_f, out_b,
          part, part_recv, act_out, back_out, pair, sq_out, sq_in,
-         raw_fwd, raw_up, raw_pair, raw_down, sems, far_sem):
+         raw_fwd, raw_up, raw_pair, raw_down, relief, sems, far_sem):
     n_sec, n_ten, n_dp, chunk = sizes
     rows, width = fwd.shape
     rank = down_hbm.shape[0]
@@ -319,8 +324,35 @@
                 + normed
                 - sav[span, cols].astype(F32) * tilt
             ).astype(BF16)
-            if first or cols in done_b[:1]:
+            if detour and first and start == groups[1][0]:
+                send_middle(start, size, cols)
+            elif first or cols in done_b[:1]:
                 shift(1, start, size, cols).start()
+
+    side = 2 * LANES
+    cut = width - raw_b - 2 * side
+    detour = bits == 2 and n_sec > 1 and len(groups) > 2 and n_dp > 1
+    odd = dp % 2 == 1
+    sender = jnp.logical_and(jnp.logical_and(sec == 1, ten == 0), odd)
+
+    def side_way(bit):
+        block = (pl.ds(*groups[1]), pl.ds(cut + bit * side, side))
+        helped = remote(out_b.at[block], relief, sem("out_b", "s"), sem("relief", "r"), tensor=flip(ten, bit))
+        given = remote(
+            relief, next_gr.at[block], sem("relief", "s"), sem("out_b", "r"), section=sec - 1, tensor=flip(ten, bit)
+        )
+        return helped, given, jnp.logical_and(jnp.logical_and(sec == 1, ten == 1 << bit), odd)
+
+    def send_middle(start, size, cols):
+        @pl.when(sender)
+        def _():
+            if cols.start < cut:
+                shift(1, start, size, slice(cols.start, min(cols.stop, cut))).start()
+            for bit in range(2):
+                if cols.start < cut + (bit + 1) * side <= cols.stop:
+                    side_way(bit)[0].start()
+
+        pl.when(jnp.logical_not(sender))(shift(1, start, size, cols).start)
 
     def send_late():
         start, size = groups[-1]
@@ -424,6 +456,15 @@
     for k in range(1, n_dp):
         trade(k).start()
 
+    if detour:
+        for bit in range(2):
+            helped, given, helper = side_way(bit)
+
+            @pl.when(helper)
+            def _():
+                helped.wait_recv()
+                given.start()
+
     @pl.when(sec == 0)
     def _():
         next_in[...] = jnp.zeros_like(next_in)
@@ -496,6 +537,11 @@
             rest = send_b.at[:, pl.ds(first_rows, rows - first_rows)]
             remote(rest, rest, sem("b_send"), sem("first", "r"), tensor=flip(ten, 0)).wait_send()
         remote(send_f, recv_f, sem("f_send"), sem("f", 0), tensor=flip(ten, 0)).wait_send()
+
+    if detour:
+        for bit in range(2):
+            helped, given, helper = side_way(bit)
+            pl.when(helper)(given.wait_send)
 
     whole_f = across(1, fwd, out_f, sem("out_f", "s"), sem("out_f", "r"))
     whole_b = across(-1, kept, out_b, sem("out_b", "s"), sem("out_b", "r"))
@@ -579,7 +625,8 @@
                 pltpu.VMEM((rank, raw_f), BF16),
                 pltpu.VMEM((2, rows, raw_b), BF16),
                 pltpu.VMEM((rank, raw_b), BF16),
-                dma((len(semaphores(len(row_groups(rows)), bits, n_dp)),)),
+                pltpu.VMEM((row_groups(rows)[1 % len(row_groups(rows))][1], 2 * LANES), BF16),
+                dma((max(semaphores(len(row_groups(rows)), bits, n_dp).values()) + 1,)),
                 pltpu.SemaphoreType.REGULAR,
             ],
             compiler_params=pltpu.CompilerParams(collective_id=0, has_side_effects=True),

time: 28.4 us -> 27.7 us (0.975)
  Pallas kernels: 27.6 us -> 26.8 us
    pallas_call x1, Pallas kernels: 26.1 us -> 25.4 us  [shards(): pl.pallas_call(functools.partial(tick, (n_sec, n_ten, n_dp, chunk)), out_...]
where the time goes in v3:
time: 27.7 us; the launch traced here: 27.5 us
  Pallas kernels  26.8 us (97%)
  between operations  0.64 us (2%)
    pallas_call x1, Pallas kernels, shards(): pl.pallas_call(functools.partial(tick, (n_sec, n_ten, n_dp, chunk)), out_...  25.4 us
    pallas_call x1, Pallas kernels, shards(): pl.pallas_call(place, out_shape=tuple((jax.ShapeDtypeStruct(shape, BF16)...  1.43 us

profile of v3, /device:TPU:1, one launch (start us, length us, event | category | flops | bytes accessed | tf_op | source)
XLA Modules:
  0.0 27.5 jit_solution(4605582955487563991)
XLA Ops:
  0.6 25.4 %tick.1 = (bf16[192,2048]{1,0:T(8,128)(2,1)S(1)}, bf16[192,2048]{1,0:T(8,128)(2,1)S(1)}, bf16[96,2048]{1,0:T(8,128)(2,1)S(1)}, bf16[96,2048]{1,0:T(8,128)(2,1)S(1)}) custom-call(bf16[192,2048]{1,0:T(8,128)(2,1)} %bitcast.10, bf16[192,2048]{1,0:T(8,128)(2,1)} %bitcast.11, bf16[192,2048]{1,0:T(8,128)(2,1)} %bitcast.12, s32[1,2]{1,0:T(1,128)} %bitcast.15, ...), custom_call_target="tpu_custom_call" | custom-call | flops 1056964608 | bytes 6291456 | tf_op jit(solution)/shard_map/tick/pallas_call | solution.py:597
  26.0 1.4 %place.1 = (bf16[192,2048]{1,0:T(8,128)(2,1)}, bf16[192,2048]{1,0:T(8,128)(2,1)}, bf16[96,2048]{1,0:T(8,128)(2,1)}, bf16[96,2048]{1,0:T(8,128)(2,1)}) custom-call(bf16[192,2048]{1,0:T(8,128)(2,1)S(1)} %get-tuple-element.12.refs_0_, bf16[192,2048]{1,0:T(8,128)(2,1)S(1)} %get-tuple-element.13.refs_1_, bf16[96,2048]{1,0:T(8,128)(2,1)S(1)} %get-tuple-element.14.refs_2_, ...), custom_call_target="tpu_custom_call" | custom-call | tf_op jit(solution)/shard_map/place/pallas_call | solution.py:640

commit v4 on v3

--- a/solution.py
+++ b/solution.py
@@ -69,7 +69,7 @@
          lens, gain, fwd, sav_down, kept_up, gained,
          acc_b, send_f, recv_f, send_b, recv_b, first_b, out_f, out_b,
          part, part_recv, act_out, back_out, pair, sq_out, sq_in,
-         raw_fwd, raw_up, raw_pair, raw_down, relief, sems, far_sem):
+         raw_fwd, raw_up, raw_pair, raw_down, relief, sems, far_sem, up_sem):
     n_sec, n_ten, n_dp, chunk = sizes
     rows, width = fwd.shape
     rank = down_hbm.shape[0]
@@ -104,10 +104,6 @@
         pl.semaphore_signal(barrier, inc=1, device_id={"tensor": peer(ten, k, bits)})
     for k in range(1, n_dp):
         pl.semaphore_signal(barrier, inc=1, device_id={"dp": (dp + k) % n_dp})
-
-    @pl.when(sec > 0)
-    def _():
-        pl.semaphore_signal(barrier, inc=1, device_id={"section": sec - 1})
 
     @pl.when(sec < n_sec - 1)
     def _():
@@ -205,7 +201,12 @@
 
     loads["sav_tail"].wait()
 
-    pl.semaphore_wait(barrier, len(near) + n_dp - 1 + jnp.where(sec > 0, 1, 0) + jnp.where(sec < n_sec - 1, 1, 0))
+    pl.semaphore_wait(barrier, len(near) + n_dp - 1 + jnp.where(sec > 0, 1, 0))
+
+    @pl.when(sec > 0)
+    def _():
+        pl.semaphore_signal(up_sem, inc=1, device_id={"section": sec - 1})
+
     if relayed:
         pl.semaphore_signal(far_sem, inc=1, device_id={"tensor": flip(ten, 0)})
 
@@ -217,7 +218,7 @@
         loads[name].wait()
     square_s = jnp.zeros((rows, 1), F32)
     total_s = jnp.zeros((rows, rank), F32)
-    for cols in columns:
+    for cols in columns[::-1]:
         values = sav[:, cols].astype(F32)
         square_s += jnp.sum(values * values, axis=1, keepdims=True)
         scaled = down[:, cols] * gain[:, cols]
@@ -233,10 +234,6 @@
 
     loads["len"].wait()
     loads["kept_up"].wait()
-
-    @pl.when(sec < n_sec - 1)
-    def _():
-        raw_ups.start()
 
     position = lax.broadcasted_iota(jnp.int32, (rows, 1), 0)
     seq_rows = rows // n_seq
@@ -261,6 +258,8 @@
 
     @pl.when(sec < n_sec - 1)
     def _():
+        pl.semaphore_wait(up_sem, 1)
+        raw_ups.start()
         raw_fwds.start()
 
     for cols in columns[::-1]:
@@ -282,8 +281,6 @@
         send_f[p, :, rank:] = spread(square_f, 3)
         exchange_f(p)
 
-    if bits:
-        begin_f(0, total, square_f)
     def step_b(p, chosen):
         for g, (start, size) in chosen:
             span = pl.ds(start, size)
@@ -296,6 +293,8 @@
     later = list(enumerate(groups))[1:]
     if bits > 1:
         step_b(1, later[:1])
+    if bits:
+        begin_f(0, total, square_f)
 
     done_f = [slice(a, min(a + chunk, width - raw_f)) for a in range(0, width - raw_f, chunk)]
     done_b = [slice(a, min(a + chunk, width - raw_b)) for a in range(0, width - raw_b, chunk)]
@@ -628,6 +627,7 @@
                 pltpu.VMEM((row_groups(rows)[1 % len(row_groups(rows))][1], 2 * LANES), BF16),
                 dma((max(semaphores(len(row_groups(rows)), bits, n_dp).values()) + 1,)),
                 pltpu.SemaphoreType.REGULAR,
+                pltpu.SemaphoreType.REGULAR,
             ],
             compiler_params=pltpu.CompilerParams(collective_id=0, has_side_effects=True),
             cost_estimate=pl.CostEstimate(

time: 27.7 us -> 27.5 us (level)
  no operation moved by 1% of the time
where the time goes in v4:
time: 27.5 us; the launch traced here: 27.3 us
  Pallas kernels  26.7 us (97%)
  between operations  0.64 us (2%)
    pallas_call x1, Pallas kernels, shards(): pl.pallas_call(functools.partial(tick, (n_sec, n_ten, n_dp, chunk)), out_...  25.3 us
    pallas_call x1, Pallas kernels, shards(): pl.pallas_call(place, out_shape=tuple((jax.ShapeDtypeStruct(shape, BF16)...  1.43 us

profile of v4, /device:TPU:1, one launch (start us, length us, event | category | flops | bytes accessed | tf_op | source)
XLA Modules:
  0.0 27.3 jit_solution(10850195765127597245)
XLA Ops:
  0.6 25.3 %tick.1 = (bf16[192,2048]{1,0:T(8,128)(2,1)S(1)}, bf16[192,2048]{1,0:T(8,128)(2,1)S(1)}, bf16[96,2048]{1,0:T(8,128)(2,1)S(1)}, bf16[96,2048]{1,0:T(8,128)(2,1)S(1)}) custom-call(bf16[192,2048]{1,0:T(8,128)(2,1)} %bitcast.10, bf16[192,2048]{1,0:T(8,128)(2,1)} %bitcast.11, bf16[192,2048]{1,0:T(8,128)(2,1)} %bitcast.12, s32[1,2]{1,0:T(1,128)} %bitcast.15, ...), custom_call_target="tpu_custom_call" | custom-call | flops 1056964608 | bytes 6291456 | tf_op jit(solution)/shard_map/tick/pallas_call | solution.py:596
  25.9 1.4 %place.1 = (bf16[192,2048]{1,0:T(8,128)(2,1)}, bf16[192,2048]{1,0:T(8,128)(2,1)}, bf16[96,2048]{1,0:T(8,128)(2,1)}, bf16[96,2048]{1,0:T(8,128)(2,1)}) custom-call(bf16[192,2048]{1,0:T(8,128)(2,1)S(1)} %get-tuple-element.12.refs_0_, bf16[192,2048]{1,0:T(8,128)(2,1)S(1)} %get-tuple-element.13.refs_1_, bf16[96,2048]{1,0:T(8,128)(2,1)S(1)} %get-tuple-element.14.refs_2_, ...), custom_call_target="tpu_custom_call" | custom-call | tf_op jit(solution)/shard_map/place/pallas_call | solution.py:640

commit v5 on v4

--- a/solution.py
+++ b/solution.py
@@ -329,27 +329,34 @@
                 shift(1, start, size, cols).start()
 
     side = 2 * LANES
-    cut = width - raw_b - 2 * side
-    detour = bits == 2 and n_sec > 1 and len(groups) > 2 and n_dp > 1
+    cut = width - raw_b - 3 * side
+    detour = bits == 2 and n_sec > 1 and len(groups) > 2 and n_dp > 1 and cut > 0
     odd = dp % 2 == 1
-    sender = jnp.logical_and(jnp.logical_and(sec == 1, ten == 0), odd)
-
-    def side_way(bit):
-        block = (pl.ds(*groups[1]), pl.ds(cut + bit * side, side))
-        helped = remote(out_b.at[block], relief, sem("out_b", "s"), sem("relief", "r"), tensor=flip(ten, bit))
+    sender = jnp.logical_and(ten == 0, odd)
+
+    def side_way(k):
+        block = (pl.ds(*groups[1]), pl.ds(cut + (k - 1) * side, side))
+        place = peer(ten, k, bits)
+        helped = remote(out_b.at[block], relief, sem("out_b", "s"), sem("relief", "r"), tensor=place)
         given = remote(
-            relief, next_gr.at[block], sem("relief", "s"), sem("out_b", "r"), section=sec - 1, tensor=flip(ten, bit)
+            relief, next_gr.at[block], sem("relief", "s"), sem("out_b", "r"), section=sec - 1, tensor=place
         )
-        return helped, given, jnp.logical_and(jnp.logical_and(sec == 1, ten == 1 << bit), odd)
+        wanted = sec > 0 if k == 3 else sec == 1
+        return helped, given, jnp.logical_and(jnp.logical_and(wanted, ten == k), odd)
 
     def send_middle(start, size, cols):
         @pl.when(sender)
         def _():
             if cols.start < cut:
                 shift(1, start, size, slice(cols.start, min(cols.stop, cut))).start()
-            for bit in range(2):
-                if cols.start < cut + (bit + 1) * side <= cols.stop:
-                    side_way(bit)[0].start()
+            for k in range(1, 4):
+                first = cut + (k - 1) * side
+                if cols.start < first + side <= cols.stop:
+                    if k == 3:
+                        side_way(k)[0].start()
+                    else:
+                        pl.when(sec == 1)(side_way(k)[0].start)
+                        pl.when(sec > 1)(shift(1, start, size, slice(first, first + side)).start)
 
         pl.when(jnp.logical_not(sender))(shift(1, start, size, cols).start)
 
@@ -456,8 +463,8 @@
         trade(k).start()
 
     if detour:
-        for bit in range(2):
-            helped, given, helper = side_way(bit)
+        for k in range(1, 4):
+            helped, given, helper = side_way(k)
 
             @pl.when(helper)
             def _():
@@ -538,8 +545,8 @@
         remote(send_f, recv_f, sem("f_send"), sem("f", 0), tensor=flip(ten, 0)).wait_send()
 
     if detour:
-        for bit in range(2):
-            helped, given, helper = side_way(bit)
+        for k in range(1, 4):
+            helped, given, helper = side_way(k)
             pl.when(helper)(given.wait_send)
 
     whole_f = across(1, fwd, out_f, sem("out_f", "s"), sem("out_f", "r"))

time: 27.5 us -> 27.4 us (level)
  no operation moved by 1% of the time
where the time goes in v5:
time: 27.4 us; the launch traced here: 27.3 us
  Pallas kernels  26.6 us (97%)
  between operations  0.64 us (2%)
    pallas_call x1, Pallas kernels, shards(): pl.pallas_call(functools.partial(tick, (n_sec, n_ten, n_dp, chunk)), out_...  25.2 us
    pallas_call x1, Pallas kernels, shards(): pl.pallas_call(place, out_shape=tuple((jax.ShapeDtypeStruct(shape, BF16)...  1.43 us

profile of v5, /device:TPU:1, one launch (start us, length us, event | category | flops | bytes accessed | tf_op | source)
XLA Modules:
  0.0 27.3 jit_solution(4360455598099310371)
XLA Ops:
  0.6 25.2 %tick.1 = (bf16[192,2048]{1,0:T(8,128)(2,1)S(1)}, bf16[192,2048]{1,0:T(8,128)(2,1)S(1)}, bf16[96,2048]{1,0:T(8,128)(2,1)S(1)}, bf16[96,2048]{1,0:T(8,128)(2,1)S(1)}) custom-call(bf16[192,2048]{1,0:T(8,128)(2,1)} %bitcast.10, bf16[192,2048]{1,0:T(8,128)(2,1)} %bitcast.11, bf16[192,2048]{1,0:T(8,128)(2,1)} %bitcast.12, s32[1,2]{1,0:T(1,128)} %bitcast.15, ...), custom_call_target="tpu_custom_call" | custom-call | flops 1056964608 | bytes 6291456 | tf_op jit(solution)/shard_map/tick/pallas_call | solution.py:603
  25.8 1.4 %place.1 = (bf16[192,2048]{1,0:T(8,128)(2,1)}, bf16[192,2048]{1,0:T(8,128)(2,1)}, bf16[96,2048]{1,0:T(8,128)(2,1)}, bf16[96,2048]{1,0:T(8,128)(2,1)}) custom-call(bf16[192,2048]{1,0:T(8,128)(2,1)S(1)} %get-tuple-element.12.refs_0_, bf16[192,2048]{1,0:T(8,128)(2,1)S(1)} %get-tuple-element.13.refs_1_, bf16[96,2048]{1,0:T(8,128)(2,1)S(1)} %get-tuple-element.14.refs_2_, ...), custom_call_target="tpu_custom_call" | custom-call | tf_op jit(solution)/shard_map/place/pallas_call | solution.py:647
